TPU v7x, 256 devices: a whole 4x4x8 slice. The times are simulated.
256 devices in a mesh: ch: 128 (over x, y_lo, z, core), rep: 2 (over y_hi).
Axes of the slice: x: 4, y: 4 (y_hi: 2, y_lo: 2; y = y_hi * 2 + y_lo), z: 8, core: 2. Of those that a mesh axis runs over, the one named last changes fastest.
Arguments:
- fields_a: bfloat16 [32, 128, 32768], P('rep', 'ch'), parts along dimension 0, may hold values from -6 to 6
- latent_b: bfloat16 [32, 16384, 512], P('rep', 'ch'), parts along dimension 0, may hold values from -6 to 6
- regrid_w: bfloat16 [256, 1, 128, 64], replicated, may hold values from -0.5 to 0.5
- cell_tiles: int32 [256, 1], replicated, may hold values from 0 to 255, as said below
- norm_a: float32 [128], replicated, may hold values from 0.5 to 1.5
- enc_in: bfloat16 [128, 512], replicated, may hold values from -0.5 to 0.5
- enc_mid: bfloat16 [512, 512], replicated, may hold values from -0.25 to 0.25
- enc_out: bfloat16 [512, 512], replicated, may hold values from -0.25 to 0.25
- norm_b: float32 [512], replicated, may hold values from 0.5 to 1.5
- dec_mid: bfloat16 [512, 512], replicated, may hold values from -0.25 to 0.25
- dec_out: bfloat16 [512, 128], replicated, may hold values from -0.25 to 0.25
Outputs:
- latent_a: bfloat16 [32, 16384, 512], P('rep', 'ch'), parts along dimension 0
- cells_b: bfloat16 [32, 128, 32768], P('rep', 'ch'), parts along dimension 0
There are 2 independent parts, one for each index of `rep`. A program takes and returns all parts, laid end to end along the dimension named above; an argument that names none is the same for every part. Nothing has to cross between parts.
Inputs may be any that keep to these rules, and one draw needn't show every extreme that they name: The one column of cell_tiles names every one of the 256 cell blocks exactly once.
All inputs are finite; a program needn't handle non-finite values.
Results may differ from a plain program's by a relative error of at most 0.0066.
Values may be sent and summed in bfloat16 or wider, within the bound.
A program may use at most 64 MiB of HBM per device.

v0:
```python
import jax
import jax.numpy as jnp
from jax import lax
from jax.sharding import PartitionSpec as P

BN = 64
BC = 128
K = 1


EPSILON = 1e-05


def normalize(values, gain_vec, along):
    average = jnp.mean(values, axis=along, keepdims=True)
    centred = values - average
    spread = jnp.mean(centred * centred, axis=along, keepdims=True)
    return centred * lax.rsqrt(spread + EPSILON) * gain_vec


def shards(
    fields_a,
    latent_b,
    regrid_w,
    cell_tiles,
    norm_a,
    enc_in,
    enc_mid,
    enc_out,
    norm_b,
    dec_mid,
    dec_out,
):
    groups = lax.axis_size("ch")
    samples = fields_a.shape[0]
    own_channels = fields_a.shape[1]
    blocks_all = cell_tiles.shape[0]
    node_rows = latent_b.shape[1]
    hidden = latent_b.shape[2]
    channels = own_channels * groups
    blocks = fields_a.reshape(samples, own_channels, blocks_all, BC)
    chosen = jnp.take(blocks, cell_tiles, axis=2).reshape(samples, own_channels, blocks_all, K * BC)
    weights = regrid_w.reshape(blocks_all, K * BC, BN)
    grid_vals = jnp.einsum("ecnj,njm->ecnm", chosen, weights, preferred_element_type=jnp.float32)
    grid_sent = grid_vals.astype(jnp.bfloat16).reshape(samples, own_channels, groups, node_rows)
    received_a = lax.all_to_all(grid_sent, "ch", split_axis=2, concat_axis=1, tiled=True)
    normed = normalize(latent_b.astype(jnp.float32), norm_b, 2).astype(jnp.bfloat16)
    middle = jax.nn.silu(
        jnp.einsum("enh,hg->eng", normed, dec_mid, preferred_element_type=jnp.float32)
    ).astype(jnp.bfloat16)
    out_split = dec_out.reshape(hidden, groups, own_channels)
    decoded_sent = jnp.einsum(
        "enh,hjc->ecjn", middle, out_split, preferred_element_type=jnp.float32
    ).astype(jnp.bfloat16)
    values = received_a.reshape(samples, channels, node_rows).astype(jnp.float32)
    normed = normalize(values, norm_a[:, None], 1).astype(jnp.bfloat16)
    base = jnp.einsum("ecn,ch->enh", normed, enc_in, preferred_element_type=jnp.float32).astype(
        jnp.bfloat16
    )
    middle = jax.nn.silu(
        jnp.einsum("enh,hg->eng", base, enc_mid, preferred_element_type=jnp.float32)
    ).astype(jnp.bfloat16)
    result = base.astype(jnp.float32) + jnp.einsum(
        "enh,hg->eng", middle, enc_out, preferred_element_type=jnp.float32
    )
    latent_a = result.astype(jnp.bfloat16)
    received_b = lax.all_to_all(decoded_sent, "ch", split_axis=2, concat_axis=1, tiled=True)
    node_blocks = jnp.moveaxis(received_b, 1, 2).reshape(samples, own_channels, blocks_all, BN)
    inverse = jnp.argsort(cell_tiles, axis=0).T
    picked = jnp.take(node_blocks, inverse, axis=2)
    weight_sel = regrid_w[inverse, jnp.arange(K)[:, None]]
    total = jnp.einsum("ecknm,knbm->ecnb", picked, weight_sel, preferred_element_type=jnp.float32)
    cells_b = total.astype(jnp.bfloat16).reshape(samples, own_channels, blocks_all * BC)
    return (latent_a, cells_b)


def solution(mesh):
    placed = (
        P("rep", "ch", None),
        P("rep", "ch", None),
        P(),
        P(),
        P(),
        P(),
        P(),
        P(),
        P(),
        P(),
        P(),
    )
    return jax.shard_map(
        shards,
        mesh=mesh,
        in_specs=placed,
        out_specs=(P("rep", "ch", None), P("rep", "ch", None)),
        check_vma=False,
    )
```

profile of v0, /device:TPU:1, one launch (start us, length us, event | category | flops | bytes accessed | tf_op | source)
XLA Modules:
  0.0 80.6 jit_solution(7968910179275049129)
XLA Ops:
  0.6 0.0 copy-start
  0.6 0.0 copy-start.1
  0.7 0.0 copy-start.6
  0.7 0.0 copy-start.7
  0.7 2.1 %convert_reduce_fusion = f32[16,128]{1,0:T(8,128)S(1)} fusion(bf16[16,128,512]{2,1,0:T(8,128)(2,1)} %param.12), kind=kLoop, calls=%fused_computation.4 | loop fusion | flops 2095104 | bytes 2105344 | tf_op jit(solution)/shard_map/reduce_sum | solution.py:15
  2.8 2.5 %fusion.2 = f32[16,128]{1,0:T(8,128)S(1)} fusion(bf16[16,128,512]{2,1,0:T(8,128)(2,1)} %param.12, f32[16,128]{1,0:T(8,128)S(1)} %broadcast_multiply_fusion), kind=kLoop, calls=%fused_computation.7 | loop fusion | flops 4192256 | bytes 2113536 | tf_op jit(solution)/shard_map/reduce_sum | solution.py:17
  5.3 0.0 copy-done.1
  5.3 0.0 copy-done.6
  5.3 0.0 copy-done.7
  5.3 3.4 %fusion.27 = bf16[16,1,128,128]{2,3,0,1:T(8,128)(2,1)S(1)} fusion(bf16[16,128,512]{2,1,0:T(8,128)(2,1)S(1)} %copy-done.1, f32[512]{0:T(512)S(1)} %copy-done.7, f32[16,128]{1,0:T(8,128)S(1)} %add_rsqrt_fusion, f32[16,128]{1,0:T(8,128)S(1)} %broadcast_multiply_fusion, bf16[512,512]{1,0:T(8,128)(2,1)} %param.20, bf16[512,128]{1,0:T(8,128)(2,1)S(1)} %copy-done.6), kind=kOutput, calls=%fused_computation.29 | convolution fusion | flops 1352925184 | bytes 3295232 | tf_op jit(solution)/shard_map/enh,hjc->ecjn/dot_general | solution.py:52
  8.7 0.0 copy-start.3
  8.7 1.2 %copy.28 = bf16[16,1,128,128]{3,0,1,2:T(8,128)(2,1)} copy(bf16[16,1,128,128]{2,3,0,1:T(8,128)(2,1)S(1)} %fusion.27) | data formatting | bytes 1048576 | tf_op jit(solution)/shard_map/convert_element_type | solution.py:54
  9.9 14.8 %all-to-all-start.1 = ((bf16[16,1,128,128]{3,0,1,2:T(8,128)(2,1)}), bf16[16,1,128,128]{3,0,1,2:T(8,128)(2,1)S(1)}, u32[]{:S(2)}, u32[]{:S(2)}) async-start(bf16[16,1,128,128]{3,0,1,2:T(8,128)(2,1)} %copy.28), calls=%async_computation.1 | async-start | bytes 1048576 | tf_op jit(solution)/shard_map/all_to_all | solution.py:67
  24.7 1.4 %copy.33 = bf16[2,8,256,128]{3,2,1,0:T(8,128)(2,1)S(1)} copy(bf16[2,8,256,128]{3,1,2,0:T(8,128)(2,1)} %bitcast.88) | data formatting | bytes 2097152
  26.1 0.7 copy.24
  26.8 0.0 copy-done.3
  26.8 0.8 %gather_fusion = bf16[256,16,128]{2,1,0:T(8,128)(2,1)S(1)} fusion(bf16[16,256,128]{2,0,1:T(8,128)(2,1)S(1)} %copy.24, s32[1024]{0:T(1024)S(1)} %pad_clamp_fusion.1), kind=kCustom, calls=%fused_computation | custom fusion | bytes 2098176 | tf_op jit(solution)/shard_map/jit(_take)/gather | solution.py:42
  27.7 4.5 %fusion.19 = bf16[16,1,256,64]{3,0,2,1:T(8,128)(2,1)S(1)} fusion(bf16[256,1,128,64]{2,3,1,0:T(8,128)(2,1)} %param.13, bf16[256,16,128]{2,1,0:T(8,128)(2,1)S(1)} %gather_fusion, pred[256]{0:T(512)(128)(4,1)S(1)} %get-tuple-element.4), kind=kOutput, calls=%fused_computation.25 | convolution fusion | flops 67895296 | bytes 5767424 | tf_op jit(solution)/shard_map/ecnj,njm->ecnm/dot_general | solution.py:44
  32.2 0.3 copy.25
  32.5 0.5 reshape.155
  33.0 1.1 %copy.26 = bf16[16,1,128,128]{3,0,1,2:T(8,128)(2,1)} copy(bf16[16,1,128,128]{3,2,0,1:T(8,128)(2,1)S(1)} %reshape.155) | data formatting | bytes 1048576 | tf_op jit(solution)/shard_map/reshape | solution.py:45
  34.1 10.5 %all-to-all-done.1 = bf16[16,1,128,128]{3,0,1,2:T(8,128)(2,1)S(1)} async-done(((bf16[16,1,128,128]{3,0,1,2:T(8,128)(2,1)}), bf16[16,1,128,128]{3,0,1,2:T(8,128)(2,1)S(1)}, u32[]{:S(2)}, u32[]{:S(2)}) %all-to-all-start.1) | async-done | bytes 524320 | tf_op jit(solution)/shard_map/all_to_all | solution.py:67
  44.6 5.5 %all-to-all-start = ((bf16[16,1,128,128]{3,0,1,2:T(8,128)(2,1)}), bf16[16,1,128,128]{3,0,1,2:T(8,128)(2,1)S(1)}, u32[]{:S(2)}, u32[]{:S(2)}) async-start(bf16[16,1,128,128]{3,0,1,2:T(8,128)(2,1)} %copy.26), calls=%async_computation | async-start | bytes 1048576 | tf_op jit(solution)/shard_map/all_to_all | solution.py:46
  50.1 3.2 %sort.17 = (s32[256,1]{0,1:T(1,128)}, s32[256,1]{0,1:T(1,128)S(1)}) sort(s32[256,1]{0,1:T(1,128)S(1)} %copy-done.3, s32[256,1]{0,1:T(1,128)S(1)} %iota.7), dimensions={0}, to_apply=%region_2.3 | sort | flops 2048 | bytes 4096 | tf_op jit(solution)/shard_map/jit(argsort)/sort | solution.py:69
  53.4 5.2 %gather_fusion.1 = bf16[256,128,64]{1,2,0:T(8,128)(2,1)} fusion(bf16[256,1,128,64]{2,3,1,0:T(8,128)(2,1)} %param.13, s32[256]{0:T(256)S(1)} %bitcast.86), kind=kCustom, calls=%fused_computation.1 | custom fusion | bytes 8390656 | tf_op jit(solution)/shard_map/gather | solution.py:71
  58.6 0.1 copy.29
  58.7 0.4 reshape.176
  59.1 0.7 copy.30
  59.8 9.9 %all-to-all-done = bf16[16,1,128,128]{3,0,1,2:T(8,128)(2,1)S(1)} async-done(((bf16[16,1,128,128]{3,0,1,2:T(8,128)(2,1)}), bf16[16,1,128,128]{3,0,1,2:T(8,128)(2,1)S(1)}, u32[]{:S(2)}, u32[]{:S(2)}) %all-to-all-start) | async-done | bytes 524320 | tf_op jit(solution)/shard_map/all_to_all | solution.py:46
  69.8 0.1 convert_reduce_fusion.1
  69.9 0.2 fusion.33
  70.1 0.9 %gather_fusion.2 = bf16[256,16,64]{2,1,0:T(8,128)(2,1)S(1)} fusion(bf16[16,256,64]{2,0,1:T(8,128)(2,1)S(1)} %copy.30, s32[1024]{0:T(1024)S(1)} %pad_clamp_fusion), kind=kCustom, calls=%fused_computation.2 | custom fusion | bytes 1049600 | tf_op jit(solution)/shard_map/jit(_take)/gather | solution.py:70
  71.0 0.0 copy-start.4
  71.0 0.0 copy-start.2
  71.0 3.5 %fusion.18 = bf16[1,256,2,8,128]{4,3,2,1,0:T(8,128)(2,1)S(1)} fusion(bf16[256,128,64]{1,2,0:T(8,128)(2,1)} %gather_fusion.1, bf16[256,16,64]{2,1,0:T(8,128)(2,1)S(1)} %gather_fusion.2, pred[256]{0:T(512)(128)(4,1)S(1)} %compare_and_fusion), kind=kOutput, calls=%fused_computation.24 | convolution fusion | flops 67895296 | bytes 5767424 | tf_op jit(solution)/shard_map/ecknm,knbm->ecnb/dot_general | solution.py:72
  74.5 0.0 copy-start.5
  74.5 1.0 %copy.37 = bf16[1,256,2,8,128]{4,3,1,2,0:T(8,128)(2,1)} copy(bf16[1,256,2,8,128]{4,3,2,1,0:T(8,128)(2,1)S(1)} %fusion.18) | data formatting | bytes 2097152 | tf_op jit(solution)/shard_map/reshape | solution.py:73
  75.5 0.0 copy-done.4
  75.5 0.2 fusion.35
  75.8 0.0 copy-done.2
  75.8 0.7 convolution_convert_fusion
  76.5 0.0 copy-done
  76.5 0.0 copy-done.5
  76.5 4.0 %add_convert_fusion = bf16[16,128,512]{2,1,0:T(8,128)(2,1)} fusion(bf16[16,128,512]{2,1,0:T(8,128)(2,1)S(1)} %convolution_convert_fusion, bf16[512,512]{1,0:T(8,128)(2,1)S(1)} %copy-done, bf16[512,512]{1,0:T(8,128)(2,1)S(1)} %copy-done.5), kind=kOutput, calls=%fused_computation.13 | convolution fusion | flops 2155872256 | bytes 5242880 | tf_op jit(solution)/shard_map/enh,hg->eng/dot_general | solution.py:63
  (12 shorter events, 0.1 us)
Async XLA Ops:
  0.6 75.9 %copy-start = (bf16[512,512]{1,0:T(8,128)(2,1)S(1)}, bf16[512,512]{1,0:T(8,128)(2,1)}, u32[]{:S(2)}) copy-start(bf16[512,512]{1,0:T(8,128)(2,1)} %param.18) | copy-start | bytes 1572868
  0.6 4.6 %copy-start.1 = (bf16[16,128,512]{2,1,0:T(8,128)(2,1)S(1)}, bf16[16,128,512]{2,1,0:T(8,128)(2,1)}, u32[]{:S(2)}) copy-start(bf16[16,128,512]{2,1,0:T(8,128)(2,1)} %param.12) | copy-start | bytes 6291460
  0.7 4.6 %copy-start.6 = (bf16[512,128]{1,0:T(8,128)(2,1)S(1)}, bf16[512,128]{1,0:T(8,128)(2,1)}, u32[]{:S(2)}) copy-start(bf16[512,128]{1,0:T(8,128)(2,1)} %param.21) | copy-start | bytes 393220
  0.7 4.6 %copy-start.7 = (f32[512]{0:T(512)S(1)}, f32[512]{0:T(512)}, u32[]{:S(2)}) copy-start(f32[512]{0:T(512)} %param.19) | copy-start | bytes 6148
  8.7 18.1 %copy-start.3 = (s32[256,1]{0,1:T(1,128)S(1)}, s32[256,1]{0,1:T(1,128)}, u32[]{:S(2)}) copy-start(s32[256,1]{0,1:T(1,128)} %param.14) | copy-start | bytes 3076
  9.9 34.7 %all-to-all-start.1 = ((bf16[16,1,128,128]{3,0,1,2:T(8,128)(2,1)}), bf16[16,1,128,128]{3,0,1,2:T(8,128)(2,1)S(1)}, u32[]{:S(2)}, u32[]{:S(2)}) async-start(bf16[16,1,128,128]{3,0,1,2:T(8,128)(2,1)} %copy.28), calls=%async_computation.1 | async-start | bytes 1048576 | tf_op jit(solution)/shard_map/all_to_all | solution.py:67
  44.6 25.2 %all-to-all-start = ((bf16[16,1,128,128]{3,0,1,2:T(8,128)(2,1)}), bf16[16,1,128,128]{3,0,1,2:T(8,128)(2,1)S(1)}, u32[]{:S(2)}, u32[]{:S(2)}) async-start(bf16[16,1,128,128]{3,0,1,2:T(8,128)(2,1)} %copy.26), calls=%async_computation | async-start | bytes 1048576 | tf_op jit(solution)/shard_map/all_to_all | solution.py:46
  71.0 4.6 %copy-start.4 = (f32[128]{0:T(128)S(1)}, f32[128]{0:T(128)}, u32[]{:S(2)}) copy-start(f32[128]{0:T(128)} %param.15) | copy-start | bytes 1540
  71.0 4.8 %copy-start.2 = (bf16[128,512]{1,0:T(8,128)(2,1)S(1)}, bf16[128,512]{1,0:T(8,128)(2,1)}, u32[]{:S(2)}) copy-start(bf16[128,512]{1,0:T(8,128)(2,1)} %param.16) | copy-start | bytes 393220
  74.5 2.0 %copy-start.5 = (bf16[512,512]{1,0:T(8,128)(2,1)S(1)}, bf16[512,512]{1,0:T(8,128)(2,1)}, u32[]{:S(2)}) copy-start(bf16[512,512]{1,0:T(8,128)(2,1)} %param.17) | copy-start | bytes 1572868
where the time goes:
time: 81 us; the launch traced here: 80.6 us
  waiting for transfers between devices  20.4 us (25%)
  starting transfers between devices  20.3 us (25%)
  matrix products  16.2 us (20%)
  local copies, waits for them, and re-layouts  14.4 us (18%)
  other arithmetic  8.38 us (10%)
  between operations  0.92 us (1%)
    all_to_all x1, starting transfers between devices, shards(): lax.all_to_all(decoded_sent, 'ch', split_axis=2, concat_axis=1, tiled=True)  14.8 us
    all_to_all x1, waiting for transfers between devices, shards(): lax.all_to_all(decoded_sent, 'ch', split_axis=2, concat_axis=1, tiled=True)  10.5 us
    all_to_all x1, waiting for transfers between devices, shards(): lax.all_to_all(grid_sent, 'ch', split_axis=2, concat_axis=1, tiled=True)  9.93 us
    all_to_all x1, starting transfers between devices, shards(): lax.all_to_all(grid_sent, 'ch', split_axis=2, concat_axis=1, tiled=True)  5.49 us
    gather x1, local copies, waits for them, and re-layouts, shards(): weight_sel = regrid_w[inverse, jnp.arange(K)[:, None]]  5.21 us
    dot_general x1, matrix products, shards(): jnp.einsum('ecnj,njm->ecnm', chosen, weights, preferred_element_type=jnp....  4.53 us
    dot_general x1, matrix products, shards(): jnp.einsum('enh,hg->eng', middle, enc_out, preferred_element_type=jnp.flo...  4.04 us
    dot_general x1, matrix products, shards(): jnp.einsum('ecknm,knbm->ecnb', picked, weight_sel, preferred_element_type...  3.5 us
  transfers between devices with their start and end apart: 2, of which 2 were waited for; matrix products, arithmetic and copies ran while one was open for 24% of the time, Pallas kernels for 0%

commit v1 on v0

--- a/solution.py
+++ b/solution.py
@@ -1,6 +1,10 @@
+import functools
+
 import jax
 import jax.numpy as jnp
 from jax import lax
+from jax.experimental import pallas as pl
+from jax.experimental.pallas import tpu as pltpu
 from jax.sharding import PartitionSpec as P
 
 BN = 64
@@ -16,6 +20,54 @@
     centred = values - average
     spread = jnp.mean(centred * centred, axis=along, keepdims=True)
     return centred * lax.rsqrt(spread + EPSILON) * gain_vec
+
+
+def exchange_body(groups, a_ref, b_ref, got_a, got_b, send_sem, recv_a, recv_b):
+    me = lax.axis_index("ch")
+    barrier = pltpu.get_barrier_semaphore()
+
+    def greet(step, carry):
+        peer = {"ch": lax.rem(me + step, groups)}
+        pl.semaphore_signal(barrier, inc=1, device_id=peer, device_id_type=pl.DeviceIdType.MESH)
+        return carry
+
+    lax.fori_loop(1, groups, greet, 0)
+    got_a[me] = a_ref[me]
+    got_b[me] = b_ref[me]
+    pl.semaphore_wait(barrier, groups - 1)
+    for sent, got, sem in ((a_ref, got_a, recv_a), (b_ref, got_b, recv_b)):
+
+        def send(step, carry):
+            peer = lax.rem(me + step, groups)
+            pltpu.make_async_remote_copy(
+                src_ref=sent.at[peer],
+                dst_ref=got.at[me],
+                send_sem=send_sem,
+                recv_sem=sem,
+                device_id={"ch": peer},
+                device_id_type=pl.DeviceIdType.MESH,
+            ).start()
+            return carry
+
+        lax.fori_loop(1, groups, send, 0)
+    for sent, got, sem in ((a_ref, got_a, recv_a), (b_ref, got_b, recv_b)):
+        most = pl.ds(0, groups - 1)
+        pltpu.make_async_copy(sent.at[most], got.at[most], sem).wait()
+        pltpu.make_async_copy(sent.at[most], got.at[most], send_sem).wait()
+
+
+def exchange(a, b):
+    groups = a.shape[0]
+    whole = pl.BlockSpec(memory_space=pltpu.VMEM)
+    return pl.pallas_call(
+        functools.partial(exchange_body, groups),
+        out_shape=[jax.ShapeDtypeStruct(a.shape, a.dtype)] * 2,
+        in_specs=[whole] * 2,
+        out_specs=[whole] * 2,
+        scratch_shapes=[pltpu.SemaphoreType.DMA] * 3,
+        compiler_params=pltpu.CompilerParams(collective_id=0, has_side_effects=True),
+        name="exchange",
+    )(a, b)
 
 
 def shards(
@@ -43,7 +95,6 @@
     weights = regrid_w.reshape(blocks_all, K * BC, BN)
     grid_vals = jnp.einsum("ecnj,njm->ecnm", chosen, weights, preferred_element_type=jnp.float32)
     grid_sent = grid_vals.astype(jnp.bfloat16).reshape(samples, own_channels, groups, node_rows)
-    received_a = lax.all_to_all(grid_sent, "ch", split_axis=2, concat_axis=1, tiled=True)
     normed = normalize(latent_b.astype(jnp.float32), norm_b, 2).astype(jnp.bfloat16)
     middle = jax.nn.silu(
         jnp.einsum("enh,hg->eng", normed, dec_mid, preferred_element_type=jnp.float32)
@@ -52,9 +103,13 @@
     decoded_sent = jnp.einsum(
         "enh,hjc->ecjn", middle, out_split, preferred_element_type=jnp.float32
     ).astype(jnp.bfloat16)
-    values = received_a.reshape(samples, channels, node_rows).astype(jnp.float32)
-    normed = normalize(values, norm_a[:, None], 1).astype(jnp.bfloat16)
-    base = jnp.einsum("ecn,ch->enh", normed, enc_in, preferred_element_type=jnp.float32).astype(
+    received_a, received_b = exchange(
+        jnp.transpose(grid_sent.reshape(samples, groups, node_rows), (1, 0, 2)),
+        jnp.transpose(decoded_sent.reshape(samples, groups, node_rows), (1, 0, 2)),
+    )
+    values = received_a.astype(jnp.float32)
+    normed = normalize(values, norm_a[:, None, None], 0).astype(jnp.bfloat16)
+    base = jnp.einsum("cen,ch->enh", normed, enc_in, preferred_element_type=jnp.float32).astype(
         jnp.bfloat16
     )
     middle = jax.nn.silu(
@@ -64,8 +119,7 @@
         "enh,hg->eng", middle, enc_out, preferred_element_type=jnp.float32
     )
     latent_a = result.astype(jnp.bfloat16)
-    received_b = lax.all_to_all(decoded_sent, "ch", split_axis=2, concat_axis=1, tiled=True)
-    node_blocks = jnp.moveaxis(received_b, 1, 2).reshape(samples, own_channels, blocks_all, BN)
+    node_blocks = jnp.moveaxis(received_b, 0, 1).reshape(samples, own_channels, blocks_all, BN)
     inverse = jnp.argsort(cell_tiles, axis=0).T
     picked = jnp.take(node_blocks, inverse, axis=2)
     weight_sel = regrid_w[inverse, jnp.arange(K)[:, None]]

time: 81 us -> 88.8 us (1.096)
  Pallas kernels: 0 us -> 39.1 us
  waiting for transfers between devices: 20.4 us -> 0 us
  starting transfers between devices: 20.3 us -> 0 us
  other arithmetic: 8.38 us -> 12.9 us
  matrix products: 16.2 us -> 20 us
  local copies, waits for them, and re-layouts: 14.4 us -> 15.4 us
    pallas_call x0 -> x1, Pallas kernels: none -> 39.1 us  [exchange(): pl.pallas_call(functools.partial(exchange_body, groups), out_shape=[jax.S...]
    all_to_all x2 -> x0, waiting for transfers between devices: 20.4 us -> none  [the longest x1 10.5 us: shards(): lax.all_to_all(decoded_sent, 'ch', split_axis=2, concat_axis=1, tiled=True)]
    all_to_all x2 -> x0, starting transfers between devices: 20.3 us -> none  [the longest x1 14.8 us: shards(): lax.all_to_all(decoded_sent, 'ch', split_axis=2, concat_axis=1, tiled=True)]
    dot_general x1, matrix products: 4.04 us -> 6.45 us  [shards(): jnp.einsum('enh,hg->eng', middle, enc_out, preferred_element_type=jnp.flo...]
    dot_general x1, matrix products: 0.73 us -> 2.09 us  [shards(): jnp.einsum('cen,ch->enh', normed, enc_in, preferred_element_type=jnp.floa...]
    dot_general x0 -> x1, local copies, waits for them, and re-layouts: none -> 1.2 us  [shards(): jnp.einsum('enh,hjc->ecjn', middle, out_split, preferred_element_type=jnp...]
    convert_element_type x1 -> x0, local copies, waits for them, and re-layouts: 1.19 us -> none  [shards(): decoded_sent = jnp.einsum('enh,hjc->ecjn', middle, out_split, preferred_e...]
    transpose x0 -> x1, local copies, waits for them, and re-layouts: none -> 1.18 us  [shards(): jnp.moveaxis(received_b, 0, 1)]
  transfers between devices with their start and end apart: 2 -> 0, of which waited for: 2 -> 0; matrix products, arithmetic and copies ran while one was open for 24% -> 0% of each run, Pallas kernels for 0% -> 0%
where the time goes in v1:
time: 88.8 us; the launch traced here: 88.3 us
  Pallas kernels  39.1 us (44%)
  matrix products  20 us (23%)
  local copies, waits for them, and re-layouts  15.4 us (17%)
  other arithmetic  12.9 us (15%)
    pallas_call x1, Pallas kernels, exchange(): pl.pallas_call(functools.partial(exchange_body, groups), out_shape=[jax.S...  39.1 us
    dot_general x1, matrix products, shards(): jnp.einsum('enh,hg->eng', middle, enc_out, preferred_element_type=jnp.flo...  6.45 us
    gather x1, local copies, waits for them, and re-layouts, shards(): weight_sel = regrid_w[inverse, jnp.arange(K)[:, None]]  5.21 us
    dot_general x1, matrix products, shards(): jnp.einsum('ecnj,njm->ecnm', chosen, weights, preferred_element_type=jnp....  4.54 us
    sort x1, other arithmetic, shards(): inverse = jnp.argsort(cell_tiles, axis=0).T  4.05 us
    reduce_sum x2, other arithmetic, normalize(): spread = jnp.mean(centred * centred, axis=along, keepdims=True)  3.68 us
    dot_general x1, matrix products, shards(): jnp.einsum('ecknm,knbm->ecnb', picked, weight_sel, preferred_element_type...  3.46 us
    dot_general x1, matrix products, shards(): jnp.einsum('enh,hjc->ecjn', middle, out_split, preferred_element_type=jnp...  3.41 us

profile of v1, /device:TPU:1, one launch (start us, length us, event | category | flops | bytes accessed | tf_op | source)
XLA Modules:
  0.0 88.3 jit_solution(13349105367927397538)
XLA Ops:
  0.6 0.0 copy-start
  0.6 0.0 copy-start.1
  0.7 0.0 copy-start.4
  0.7 0.0 copy-start.5
  0.7 4.1 %sort.17 = (s32[256,1]{0,1:T(1,128)}, s32[256,1]{0,1:T(1,128)S(1)}) sort(s32[256,1]{0,1:T(1,128)} %param.14, s32[256,1]{0,1:T(1,128)S(1)} %iota.7), dimensions={0}, to_apply=%region_4.5 | sort | flops 2048 | bytes 4096 | tf_op jit(solution)/shard_map/jit(argsort)/sort | solution.py:123
  4.8 0.7 and_reduce_fusion
  5.5 1.9 %convert_reduce_fusion = f32[16,128]{1,0:T(8,128)S(1)} fusion(bf16[16,128,512]{2,1,0:T(8,128)(2,1)} %param.12), kind=kLoop, calls=%fused_computation.4 | loop fusion | flops 2095104 | bytes 2105344 | tf_op jit(solution)/shard_map/reduce_sum | solution.py:19
  7.5 2.5 %fusion.2 = f32[16,128]{1,0:T(8,128)S(1)} fusion(bf16[16,128,512]{2,1,0:T(8,128)(2,1)} %param.12, f32[16,128]{1,0:T(8,128)S(1)} %broadcast_multiply_fusion.1), kind=kLoop, calls=%fused_computation.7 | loop fusion | flops 4192256 | bytes 2113536 | tf_op jit(solution)/shard_map/reduce_sum | solution.py:21
  9.9 0.0 copy-done.1
  10.0 0.0 copy-done.4
  10.0 0.0 copy-done.5
  10.0 3.4 %fusion.12 = bf16[16,128,128]{2,1,0:T(8,128)(2,1)S(1)} fusion(bf16[16,128,512]{2,1,0:T(8,128)(2,1)S(1)} %copy-done.1, f32[512]{0:T(512)S(1)} %copy-done.5, f32[16,128]{1,0:T(8,128)S(1)} %add_rsqrt_fusion.1, f32[16,128]{1,0:T(8,128)S(1)} %broadcast_multiply_fusion.1, bf16[512,512]{1,0:T(8,128)(2,1)} %param.20, bf16[512,128]{1,0:T(8,128)(2,1)S(1)} %copy-done.4), kind=kOutput, calls=%fused_computation.19 | convolution fusion | flops 1352663040 | bytes 3295232 | tf_op jit(solution)/shard_map/enh,hjc->ecjn/dot_general | solution.py:103
  13.4 1.2 %copy.25 = bf16[16,128,128]{1,0,2:T(8,128)(2,1)} copy(bf16[16,128,128]{2,1,0:T(8,128)(2,1)S(1)} %fusion.12) | data formatting | bytes 1048576 | tf_op jit(solution)/shard_map/enh,hjc->ecjn/dot_general | solution.py:103
  14.6 1.4 %copy.31 = bf16[2,8,256,128]{3,2,1,0:T(8,128)(2,1)S(1)} copy(bf16[2,8,256,128]{3,1,2,0:T(8,128)(2,1)} %bitcast.73) | data formatting | bytes 2097152
  16.0 0.7 copy.22
  16.7 0.8 gather_fusion
  17.5 4.5 %fusion.19 = bf16[16,1,256,64]{3,0,2,1:T(8,128)(2,1)S(1)} fusion(bf16[256,1,128,64]{2,3,1,0:T(8,128)(2,1)} %param.13, bf16[256,16,128]{2,1,0:T(8,128)(2,1)S(1)} %gather_fusion, pred[256]{0:T(512)(128)(4,1)S(1)} %get-tuple-element.8), kind=kOutput, calls=%fused_computation.25 | convolution fusion | flops 67895296 | bytes 5767424 | tf_op jit(solution)/shard_map/ecnj,njm->ecnm/dot_general | solution.py:96
  22.1 0.0 copy-start.3
  22.1 0.3 copy.23
  22.4 0.5 reshape_reshape.3
  22.9 1.1 %copy.37 = bf16[16,128,128]{2,0,1:T(8,128)(2,1)} copy(bf16[16,128,128]{2,1,0:T(8,128)(2,1)S(1)} %reshape_reshape.3) | data formatting | bytes 1048576 | tf_op jit(solution)/shard_map/reshape;reshape | solution.py:107
  24.0 39.1 %exchange.1 = (bf16[128,16,128]{2,1,0:T(8,128)(2,1)}, bf16[128,16,128]{2,1,0:T(8,128)(2,1)}) custom-call(bf16[128,16,128]{2,1,0:T(8,128)(2,1)} %bitcast.72, bf16[128,16,128]{2,1,0:T(8,128)(2,1)} %bitcast.71), custom_call_target="tpu_custom_call" | custom-call | tf_op jit(solution)/shard_map/exchange/pallas_call | solution.py:62
  63.1 1.2 %copy.27 = bf16[16,128,128]{2,1,0:T(8,128)(2,1)S(1)} copy(bf16[16,128,128]{2,0,1:T(8,128)(2,1)} %bitcast.75) | data formatting | bytes 1048576 | tf_op jit(solution)/shard_map/transpose | solution.py:122
  64.3 0.0 copy-start.2
  64.3 1.2 %convert_reduce_fusion.1 = f32[16,128]{1,0:T(8,128)S(1)} fusion(bf16[128,16,128]{2,1,0:T(8,128)(2,1)} %get-tuple-element.5), kind=kLoop, calls=%fused_computation.27 | loop fusion | flops 522240 | bytes 532480 | tf_op jit(solution)/shard_map/reduce_sum | solution.py:19
  65.5 1.2 %fusion.28 = f32[16,128]{1,0:T(8,128)S(1)} fusion(bf16[128,16,128]{2,1,0:T(8,128)(2,1)} %get-tuple-element.5, f32[16,128]{1,0:T(8,128)S(1)} %broadcast_multiply_fusion), kind=kLoop, calls=%fused_computation.30 | loop fusion | flops 1046528 | bytes 540672 | tf_op jit(solution)/shard_map/reduce_sum | solution.py:21
  66.8 0.0 copy-done.3
  66.8 1.3 %fusion.30 = bf16[128,16,128]{2,1,0:T(8,128)(2,1)S(1)} fusion(bf16[128,16,128]{2,1,0:T(8,128)(2,1)} %get-tuple-element.5, f32[128]{0:T(128)S(1)} %copy-done.3, f32[16,128]{1,0:T(8,128)S(1)} %add_rsqrt_fusion, f32[16,128]{1,0:T(8,128)S(1)} %broadcast_multiply_fusion), kind=kLoop, calls=%fused_computation.32 | loop fusion | flops 1310720 | bytes 1065472 | tf_op jit(solution)/shard_map/convert_element_type | solution.py:111
  68.1 0.4 reshape.167
  68.5 0.7 copy.28
  69.2 0.8 gather_fusion.2
  70.0 0.0 copy-done.2
  70.0 2.1 %convolution_convert_fusion = bf16[16,128,512]{2,1,0:T(8,128)(2,1)} fusion(bf16[128,16,128]{2,1,0:T(8,128)(2,1)S(1)} %fusion.30, bf16[128,512]{1,0:T(8,128)(2,1)S(1)} %copy-done.2), kind=kOutput, calls=%fused_computation.20 | convolution fusion | flops 269484032 | bytes 2752512 | tf_op jit(solution)/shard_map/cen,ch->enh/dot_general | solution.py:112
  72.1 0.0 copy-done
  72.1 6.5 %add_convert_fusion = bf16[16,128,512]{2,1,0:T(8,128)(2,1)} fusion(bf16[16,128,512]{2,1,0:T(8,128)(2,1)} %convolution_convert_fusion, bf16[512,512]{1,0:T(8,128)(2,1)S(1)} %copy-done, bf16[512,512]{1,0:T(8,128)(2,1)} %param.17), kind=kOutput, calls=%fused_computation.12 | convolution fusion | flops 2155872256 | bytes 5242880 | tf_op jit(solution)/shard_map/enh,hg->eng/dot_general | solution.py:118
  78.6 5.2 %gather_fusion.1 = bf16[256,128,64]{1,2,0:T(8,128)(2,1)} fusion(bf16[256,1,128,64]{2,3,1,0:T(8,128)(2,1)} %param.13, s32[256]{0:T(256)S(1)} %bitcast.69), kind=kCustom, calls=%fused_computation.1 | custom fusion | bytes 8390656 | tf_op jit(solution)/shard_map/gather | solution.py:125
  83.8 3.5 %fusion.18 = bf16[1,256,2,8,128]{4,3,2,1,0:T(8,128)(2,1)S(1)} fusion(bf16[256,128,64]{1,2,0:T(8,128)(2,1)} %gather_fusion.1, bf16[256,16,64]{2,1,0:T(8,128)(2,1)S(1)} %gather_fusion.2, pred[256]{0:T(512)(128)(4,1)S(1)} %compare_and_fusion), kind=kOutput, calls=%fused_computation.24 | convolution fusion | flops 67895296 | bytes 5767424 | tf_op jit(solution)/shard_map/ecknm,knbm->ecnb/dot_general | solution.py:126
  87.2 1.0 %copy.36 = bf16[1,256,2,8,128]{4,3,1,2,0:T(8,128)(2,1)} copy(bf16[1,256,2,8,128]{4,3,2,1,0:T(8,128)(2,1)S(1)} %fusion.18) | data formatting | bytes 2097152 | tf_op jit(solution)/shard_map/reshape | solution.py:127
  (11 shorter events, 0.1 us)
Async XLA Ops:
  0.6 71.5 %copy-start = (bf16[512,512]{1,0:T(8,128)(2,1)S(1)}, bf16[512,512]{1,0:T(8,128)(2,1)}, u32[]{:S(2)}) copy-start(bf16[512,512]{1,0:T(8,128)(2,1)} %param.18) | copy-start | bytes 1572868
  0.6 9.3 %copy-start.1 = (bf16[16,128,512]{2,1,0:T(8,128)(2,1)S(1)}, bf16[16,128,512]{2,1,0:T(8,128)(2,1)}, u32[]{:S(2)}) copy-start(bf16[16,128,512]{2,1,0:T(8,128)(2,1)} %param.12) | copy-start | bytes 6291460
  0.7 9.3 %copy-start.4 = (bf16[512,128]{1,0:T(8,128)(2,1)S(1)}, bf16[512,128]{1,0:T(8,128)(2,1)}, u32[]{:S(2)}) copy-start(bf16[512,128]{1,0:T(8,128)(2,1)} %param.21) | copy-start | bytes 393220
  0.7 9.3 %copy-start.5 = (f32[512]{0:T(512)S(1)}, f32[512]{0:T(512)}, u32[]{:S(2)}) copy-start(f32[512]{0:T(512)} %param.19) | copy-start | bytes 6148
  22.1 44.7 %copy-start.3 = (f32[128]{0:T(128)S(1)}, f32[128]{0:T(128)}, u32[]{:S(2)}) copy-start(f32[128]{0:T(128)} %param.15) | copy-start | bytes 1540
  64.3 5.7 %copy-start.2 = (bf16[128,512]{1,0:T(8,128)(2,1)S(1)}, bf16[128,512]{1,0:T(8,128)(2,1)}, u32[]{:S(2)}) copy-start(bf16[128,512]{1,0:T(8,128)(2,1)} %param.16) | copy-start | bytes 393220

commit v2 on v0

v2 whole, which is shorter than its diff:
```python
import functools

import jax
import jax.numpy as jnp
from jax import lax
from jax.experimental import pallas as pl
from jax.experimental.pallas import tpu as pltpu
from jax.sharding import PartitionSpec as P

BN = 64
BC = 128
EPSILON = 1e-05
BATCH = 8
CHUNK = 16
PITCH_A = 24
PITCH_B = 136
NT = (((1,), (1,)), ((), ()))
MESH = pl.DeviceIdType.MESH


in_hbm = functools.partial(pltpu.with_memory_space_constraint, memory_space=pltpu.HBM)
in_vmem = functools.partial(pltpu.with_memory_space_constraint, memory_space=pltpu.VMEM)


def silu(v):
    return v / (1.0 + jnp.exp(-v))


def main_body(
    groups,
    tiles_h,
    fields_h,
    regrid_h,
    latent_h,
    norm_a_h,
    enc_in_h,
    enc_mid_h,
    enc_out_h,
    norm_b_h,
    dec_mid_h,
    dec_out_h,
    latent_o,
    cells_o,
    tiles,
    norm_a,
    fields,
    regrid,
    latent,
    enc_in,
    enc_mid,
    enc_out,
    norm_b,
    dec_mid,
    dec_out,
    sent_a,
    sent_b,
    got_a,
    got_b,
    stage_a,
    stage_b,
    load_sem,
    regrid_sem,
    send_sem,
    recv_a,
    recv_b,
):
    me = lax.axis_index("ch")
    samples, nodes = latent.shape[:2]
    chunks = groups // CHUNK
    batches = groups // BATCH

    def load(k, src, dst):
        copy = pltpu.make_async_copy(src, dst, load_sem.at[k])
        copy.start()
        return copy

    load_tiles = load(0, tiles_h, tiles)
    load_fields = load(1, fields_h, fields)
    load_regrid = []
    for k in range(chunks):
        part = pl.ds(lax.rem(me // CHUNK + k, chunks) * CHUNK, CHUNK)
        copy = pltpu.make_async_copy(regrid_h.at[part], regrid.at[part], regrid_sem.at[k])
        copy.start()
        load_regrid.append(copy)
    load_dec = [
        load(2, latent_h, latent),
        load(3, norm_b_h, norm_b),
        load(4, dec_mid_h, dec_mid),
        load(5, dec_out_h, dec_out),
    ]
    load_enc = [
        load(6, norm_a_h, norm_a),
        load(7, enc_in_h, enc_in),
        load(8, enc_mid_h, enc_mid),
        load(9, enc_out_h, enc_out),
    ]

    barrier = pltpu.get_barrier_semaphore()

    def greet(step, carry):
        peer = {"ch": lax.rem(me + step, groups)}
        pl.semaphore_signal(barrier, inc=1, device_id=peer, device_id_type=MESH)
        return carry

    lax.fori_loop(1, groups, greet, 0)

    left_half = lax.broadcasted_iota(jnp.int32, (samples, BC), 1) < BN

    def send(sent, got, sem_of):
        def one(step, carry):
            peer = lax.rem(me + step, groups)
            pltpu.make_async_remote_copy(
                src_ref=sent.at[peer],
                dst_ref=got.at[me],
                send_sem=send_sem,
                recv_sem=sem_of(step),
                device_id={"ch": peer},
                device_id_type=MESH,
            ).start()
            return carry

        return one

    send_a = send(sent_a, got_a, lambda step: recv_a)
    send_b = send(sent_b, got_b, lambda step: recv_b.at[step // BATCH])

    def regrid_batch(batch):
        for j in range(BATCH):
            d = lax.rem(me + batch * BATCH + j, groups)
            blocks = [tiles[2 * d], tiles[2 * d + 1]]
            x = [fields[rows, block] for block in blocks for rows in range(fields.shape[0])]
            both = lax.dot_general(
                jnp.concatenate(x, axis=0), regrid[d], NT, preferred_element_type=jnp.float32
            )
            mine = jnp.where(left_half, both[:samples], both[samples:])
            sent_a[d] = mine.astype(jnp.bfloat16)

    load_tiles.wait()
    load_fields.wait()
    load_regrid[0].wait()
    half_way = batches // 2
    per_chunk = CHUNK // BATCH
    for batch in range(half_way):
        if batch % per_chunk == 0:
            load_regrid[batch // per_chunk + 1].wait()
        regrid_batch(batch)
    got_a[me] = sent_a[me]
    pl.semaphore_wait(barrier, groups - 1)
    for batch in range(half_way, batches):
        if batch % per_chunk == 0 and batch // per_chunk + 1 < chunks:
            load_regrid[batch // per_chunk + 1].wait()
        regrid_batch(batch)
        done = 2 * (batch - half_way) * BATCH
        lax.fori_loop(max(1, done - BATCH), done + BATCH, send_a, 0)
    lax.fori_loop(groups - BATCH, groups, send_a, 0)

    for copy in load_dec:
        copy.wait()

    def decode(e, carry):
        v = latent[e].astype(jnp.float32)
        centred = v - jnp.mean(v, axis=1, keepdims=True)
        spread = jnp.mean(centred * centred, axis=1, keepdims=True)
        normed = (centred * lax.rsqrt(spread + EPSILON) * norm_b[...]).astype(jnp.bfloat16)
        middle = silu(jnp.dot(normed, dec_mid[...], preferred_element_type=jnp.float32))
        out = jnp.dot(
            middle.astype(jnp.bfloat16), dec_out[...], preferred_element_type=jnp.float32
        )
        stage_b[pl.ds(pl.multiple_of(e * PITCH_B, 8), groups), :] = out.T
        return carry

    lax.fori_loop(0, samples, decode, 0)

    def pack_batch(batch, carry):
        for j in range(BATCH):
            c = lax.rem(me + batch * BATCH + j, groups)
            rows = stage_b[pl.ds(c, samples, stride=PITCH_B), :]
            sent_b[c] = rows.astype(jnp.bfloat16)
        lax.fori_loop(
            jnp.maximum(1, (batch - 1) * BATCH), jnp.maximum(1, batch * BATCH), send_b, 0
        )
        return carry

    lax.fori_loop(0, batches, pack_batch, 0)
    lax.fori_loop(groups - BATCH, groups, send_b, 0)
    got_b[me] = sent_b[me]

    for copy in load_enc:
        copy.wait()
    most = pl.ds(0, groups - 1)
    pltpu.make_async_copy(sent_a.at[most], got_a.at[most], recv_a).wait()

    def add(c, total):
        return total + got_a[c].astype(jnp.float32)

    zero = jnp.zeros((samples, nodes), jnp.float32)
    average = lax.fori_loop(0, groups, add, zero, unroll=8) / groups

    def add_square(c, total):
        centred = got_a[c].astype(jnp.float32) - average
        return total + centred * centred

    spread = lax.fori_loop(0, groups, add_square, zero, unroll=8) / groups
    factor = lax.rsqrt(spread + EPSILON)

    def scale(c, carry):
        centred = got_a[c].astype(jnp.float32) - average
        rows = pl.ds(pl.multiple_of(c * PITCH_A, 8), samples)
        stage_a[rows, :] = centred * factor * norm_a[c]
        return carry

    lax.fori_loop(0, groups, scale, 0, unroll=8)

    def encode(e, carry):
        normed = stage_a[pl.ds(e, groups, stride=PITCH_A), :].T.astype(jnp.bfloat16)
        base = jnp.dot(normed, enc_in[...], preferred_element_type=jnp.float32).astype(jnp.bfloat16)
        middle = silu(jnp.dot(base, enc_mid[...], preferred_element_type=jnp.float32))
        out = base.astype(jnp.float32) + jnp.dot(
            middle.astype(jnp.bfloat16), enc_out[...], preferred_element_type=jnp.float32
        )
        latent_o[e] = out.astype(jnp.bfloat16)
        return carry

    lax.fori_loop(0, samples, encode, 0)

    def regrid_back(batch, carry):
        for j in range(BATCH):
            s = lax.rem(me + groups - batch * BATCH - j, groups)
            x = got_b[s]
            none = jnp.zeros_like(x)
            split = jnp.concatenate([jnp.where(left_half, x, none), jnp.where(left_half, none, x)], axis=0)
            cells = jnp.dot(split, regrid[s], preferred_element_type=jnp.float32)
            cells_o[s] = cells.astype(jnp.bfloat16)
        return carry

    def wait_back(batch, count):
        part = pl.ds(0, count)
        pltpu.make_async_copy(sent_b.at[part], got_b.at[part], recv_b.at[batch]).wait()

    wait_back(0, BATCH - 1)
    regrid_back(0, 0)

    def back(batch, carry):
        wait_back(batch, BATCH)
        return regrid_back(batch, carry)

    lax.fori_loop(1, batches, back, 0)
    for sent, got in ((sent_a, got_a), (sent_b, got_b)):
        pltpu.make_async_copy(sent.at[most], got.at[most], send_sem).wait()


def finish_body(tiles_h, latent, cells, latent_o, cells_o, tiles, tiles_sem, latent_sem, cells_sem):
    load = pltpu.make_async_copy(tiles_h, tiles, tiles_sem)
    load.start()
    whole = pltpu.make_async_copy(latent, latent_o, latent_sem)
    whole.start()
    load.wait()

    def place(s, carry):
        for half in range(2):
            to = pl.ds(pl.multiple_of(tiles[2 * s + half] * BC, BC), BC)
            rows = pl.ds(half * latent.shape[0], latent.shape[0])
            pltpu.make_async_copy(cells.at[s, rows], cells_o.at[:, to], cells_sem).start()
        return carry

    lax.fori_loop(0, cells.shape[0], place, 0, unroll=8)
    pltpu.make_async_copy(cells_o, cells_o, cells_sem).wait()
    whole.wait()


def shards(
    fields_a,
    latent_b,
    regrid_w,
    cell_tiles,
    norm_a,
    enc_in,
    enc_mid,
    enc_out,
    norm_b,
    dec_mid,
    dec_out,
):
    groups = lax.axis_size("ch")
    samples, nodes, hidden = latent_b.shape
    all_cells = fields_a.shape[2]
    bf16, f32 = jnp.bfloat16, jnp.float32
    tiles = cell_tiles.reshape(-1)
    fields = jnp.swapaxes(fields_a.reshape(samples // 8, 8, all_cells // BC, BC), 1, 2)
    regrid = jnp.swapaxes(regrid_w, 2, 3).reshape(groups, 2 * BN, BC)
    args = (
        tiles,
        fields,
        regrid,
        latent_b,
        norm_a,
        enc_in,
        enc_mid,
        enc_out,
        norm_b.reshape(1, -1),
        dec_mid,
        dec_out,
    )
    hbm = pl.BlockSpec(memory_space=pltpu.HBM)
    vmem = pl.BlockSpec(memory_space=pltpu.VMEM)
    message = pltpu.VMEM((groups, samples, nodes), bf16)
    latent_a, cells = pl.pallas_call(
        functools.partial(main_body, groups),
        out_shape=[
            pltpu.VMEM((samples, nodes, hidden), bf16),
            pltpu.VMEM((groups, 2 * samples, BC), bf16),
        ],
        in_specs=[hbm] * 11,
        out_specs=[vmem] * 2,
        scratch_shapes=[
            pltpu.SMEM(tiles.shape, jnp.int32),
            pltpu.SMEM(norm_a.shape, f32),
            pltpu.VMEM(fields.shape, bf16),
            pltpu.VMEM(regrid.shape, bf16),
            pltpu.VMEM(latent_b.shape, bf16),
            pltpu.VMEM(enc_in.shape, bf16),
            pltpu.VMEM(enc_mid.shape, bf16),
            pltpu.VMEM(enc_out.shape, bf16),
            pltpu.VMEM((1, hidden), f32),
            pltpu.VMEM(dec_mid.shape, bf16),
            pltpu.VMEM(dec_out.shape, bf16),
            message,
            message,
            message,
            message,
            pltpu.VMEM((groups * PITCH_A, nodes), f32),
            pltpu.VMEM((samples * PITCH_B, nodes), f32),
            pltpu.SemaphoreType.DMA((10,)),
            pltpu.SemaphoreType.DMA((groups // CHUNK,)),
            pltpu.SemaphoreType.DMA,
            pltpu.SemaphoreType.DMA,
            pltpu.SemaphoreType.DMA((groups // BATCH,)),
        ],
        compiler_params=pltpu.CompilerParams(
            collective_id=0, has_side_effects=True, vmem_limit_bytes=40 * 2**20
        ),
        name="main",
    )(*map(in_hbm, args))
    latent_a, cells_b = pl.pallas_call(
        finish_body,
        out_shape=[
            pltpu.HBM(latent_a.shape, bf16),
            pltpu.HBM((samples, all_cells), bf16),
        ],
        in_specs=[hbm, vmem, vmem],
        out_specs=[hbm, hbm],
        scratch_shapes=[
            pltpu.SMEM(tiles.shape, jnp.int32),
            pltpu.SemaphoreType.DMA,
            pltpu.SemaphoreType.DMA,
            pltpu.SemaphoreType.DMA,
        ],
        name="finish",
    )(in_hbm(tiles), in_vmem(latent_a), in_vmem(cells))
    return latent_a, cells_b.reshape(samples, 1, all_cells)


def solution(mesh):
    sharded = P("rep", "ch", None)
    return jax.shard_map(
        shards,
        mesh=mesh,
        in_specs=(sharded, sharded) + (P(),) * 9,
        out_specs=(sharded, sharded),
        check_vma=False,
    )
```

time: 81 us -> 45.3 us (0.56)
  Pallas kernels: 0 us -> 44.5 us
  waiting for transfers between devices: 20.4 us -> 0 us
  starting transfers between devices: 20.3 us -> 0 us
  matrix products: 16.2 us -> 0 us
  local copies, waits for them, and re-layouts: 14.4 us -> 0 us
  other arithmetic: 8.38 us -> 0 us
    pallas_call x0 -> x2, Pallas kernels: none -> 44.5 us  [the longest x1 42.3 us: shards(): pl.pallas_call(functools.partial(main_body, groups), out_shape=[pltpu.VME...]
    all_to_all x2 -> x0, waiting for transfers between devices: 20.4 us -> none  [the longest x1 10.5 us: shards(): lax.all_to_all(decoded_sent, 'ch', split_axis=2, concat_axis=1, tiled=True)]
    all_to_all x2 -> x0, starting transfers between devices: 20.3 us -> none  [the longest x1 14.8 us: shards(): lax.all_to_all(decoded_sent, 'ch', split_axis=2, concat_axis=1, tiled=True)]
    dot_general x5 -> x0, matrix products: 16.2 us -> none  [the longest x1 4.53 us: shards(): jnp.einsum('ecnj,njm->ecnm', chosen, weights, preferred_element_type=jnp....]
    gather x3 -> x0, local copies, waits for them, and re-layouts: 6.91 us -> none  [the longest x1 5.21 us: shards(): weight_sel = regrid_w[inverse, jnp.arange(K)[:, None]]]
    reduce_sum x4 -> x0, other arithmetic: 4.87 us -> none  [the longest x2 2.64 us: normalize(): spread = jnp.mean(centred * centred, axis=along, keepdims=True)]
    reshape x4 -> x0, local copies, waits for them, and re-layouts: 3.33 us -> none  [the longest x2 1.61 us: shards(): grid_vals.astype(jnp.bfloat16)]
    sort x1 -> x0, other arithmetic: 3.23 us -> none  [shards(): inverse = jnp.argsort(cell_tiles, axis=0).T]
  transfers between devices with their start and end apart: 2 -> 0, of which waited for: 2 -> 0; matrix products, arithmetic and copies ran while one was open for 24% -> 0% of each run, Pallas kernels for 0% -> 0%
where the time goes in v2:
time: 45.3 us; the launch traced here: 45.2 us
  Pallas kernels  44.5 us (98%)
  between operations  0.64 us (1%)
    pallas_call x1, Pallas kernels, shards(): pl.pallas_call(functools.partial(main_body, groups), out_shape=[pltpu.VME...  42.3 us
    pallas_call x1, Pallas kernels, shards(): pl.pallas_call(finish_body, out_shape=[pltpu.HBM(latent_a.shape, bf16), p...  2.25 us

profile of v2, /device:TPU:1, one launch (start us, length us, event | category | flops | bytes accessed | tf_op | source)
XLA Modules:
  0.0 45.2 jit_solution(2027568187568741647)
XLA Ops:
  0.6 42.3 %main.1 = (bf16[16,128,512]{2,1,0:T(8,128)(2,1)S(1)}, bf16[128,32,128]{2,1,0:T(8,128)(2,1)S(1)}) custom-call(s32[256]{0:T(256)} %bitcast.11, bf16[2,256,8,128]{3,2,1,0:T(8,128)(2,1)} %bitcast.10, bf16[128,128,128]{2,1,0:T(8,128)(2,1)} %bitcast.9, bf16[16,128,512]{2,1,0:T(8,128)(2,1)} %latent_h.1, f32[128]{0:T(128)} %norm_a_h.1, bf16[128,512]{1,0:T(8,128)(2,1)} %enc_in_h.1, ...), custom_call_target="tpu_custom_call" | custom-call | tf_op jit(solution)/shard_map/main/pallas_call | solution.py:307
  42.9 2.3 %finish.1 = (bf16[16,128,512]{2,1,0:T(8,128)(2,1)}, bf16[16,32768]{1,0:T(8,128)(2,1)}) custom-call(s32[256]{0:T(256)} %bitcast.12, bf16[16,128,512]{2,1,0:T(8,128)(2,1)S(1)} %get-tuple-element.6.latent, bf16[128,32,128]{2,1,0:T(8,128)(2,1)S(1)} %get-tuple-element.7.cells), custom_call_target="tpu_custom_call" | custom-call | tf_op jit(solution)/shard_map/finish/pallas_call | solution.py:344

commit v3 on v2

--- a/solution.py
+++ b/solution.py
@@ -11,6 +11,7 @@
 BC = 128
 EPSILON = 1e-05
 BATCH = 8
+TOGETHER = 4
 CHUNK = 16
 PITCH_A = 24
 PITCH_B = 136
@@ -23,7 +24,8 @@
 
 
 def silu(v):
-    return v / (1.0 + jnp.exp(-v))
+    half = 0.5 * v
+    return half + half * jnp.tanh(half)
 
 
 def main_body(
@@ -102,7 +104,7 @@
         pl.semaphore_signal(barrier, inc=1, device_id=peer, device_id_type=MESH)
         return carry
 
-    lax.fori_loop(1, groups, greet, 0)
+    lax.fori_loop(1, groups, greet, 0, unroll=8)
 
     left_half = lax.broadcasted_iota(jnp.int32, (samples, BC), 1) < BN
 
@@ -138,27 +140,30 @@
     load_tiles.wait()
     load_fields.wait()
     load_regrid[0].wait()
-    half_way = batches // 2
+    ahead = batches // 4
     per_chunk = CHUNK // BATCH
-    for batch in range(half_way):
+    for batch in range(ahead):
         if batch % per_chunk == 0:
             load_regrid[batch // per_chunk + 1].wait()
         regrid_batch(batch)
     got_a[me] = sent_a[me]
     pl.semaphore_wait(barrier, groups - 1)
-    for batch in range(half_way, batches):
+    sent = 0
+    for batch in range(ahead, batches):
         if batch % per_chunk == 0 and batch // per_chunk + 1 < chunks:
             load_regrid[batch // per_chunk + 1].wait()
         regrid_batch(batch)
-        done = 2 * (batch - half_way) * BATCH
-        lax.fori_loop(max(1, done - BATCH), done + BATCH, send_a, 0)
-    lax.fori_loop(groups - BATCH, groups, send_a, 0)
+        ready = min(batch, sent + 2)
+        lax.fori_loop(max(1, sent * BATCH), ready * BATCH, send_a, 0, unroll=True)
+        sent = ready
+    lax.fori_loop(sent * BATCH, groups, send_a, 0, unroll=True)
 
     for copy in load_dec:
         copy.wait()
 
-    def decode(e, carry):
-        v = latent[e].astype(jnp.float32)
+    def decode(block, carry):
+        first = block * TOGETHER
+        v = latent[pl.ds(first, TOGETHER)].astype(jnp.float32).reshape(TOGETHER * nodes, -1)
         centred = v - jnp.mean(v, axis=1, keepdims=True)
         spread = jnp.mean(centred * centred, axis=1, keepdims=True)
         normed = (centred * lax.rsqrt(spread + EPSILON) * norm_b[...]).astype(jnp.bfloat16)
@@ -166,23 +171,31 @@
         out = jnp.dot(
             middle.astype(jnp.bfloat16), dec_out[...], preferred_element_type=jnp.float32
         )
-        stage_b[pl.ds(pl.multiple_of(e * PITCH_B, 8), groups), :] = out.T
-        return carry
-
-    lax.fori_loop(0, samples, decode, 0)
+        for k in range(TOGETHER):
+            rows = pl.ds(pl.multiple_of((first + k) * PITCH_B, 8), groups)
+            stage_b[rows, :] = out[k * nodes : (k + 1) * nodes].T
+        return carry
+
+    lax.fori_loop(0, samples // TOGETHER, decode, 0)
 
     def pack_batch(batch, carry):
         for j in range(BATCH):
             c = lax.rem(me + batch * BATCH + j, groups)
             rows = stage_b[pl.ds(c, samples, stride=PITCH_B), :]
             sent_b[c] = rows.astype(jnp.bfloat16)
-        lax.fori_loop(
-            jnp.maximum(1, (batch - 1) * BATCH), jnp.maximum(1, batch * BATCH), send_b, 0
-        )
-        return carry
-
-    lax.fori_loop(0, batches, pack_batch, 0)
-    lax.fori_loop(groups - BATCH, groups, send_b, 0)
+        return carry
+
+    def pack_and_send(batch, carry):
+        pack_batch(batch, carry)
+        for j in range(BATCH):
+            send_b((batch - 1) * BATCH + j, carry)
+        return carry
+
+    pack_batch(0, 0)
+    pack_batch(1, 0)
+    lax.fori_loop(1, BATCH, send_b, 0, unroll=True)
+    lax.fori_loop(2, batches, pack_and_send, 0)
+    lax.fori_loop(groups - BATCH, groups, send_b, 0, unroll=True)
     got_b[me] = sent_b[me]
 
     for copy in load_enc:
@@ -211,17 +224,21 @@
 
     lax.fori_loop(0, groups, scale, 0, unroll=8)
 
-    def encode(e, carry):
-        normed = stage_a[pl.ds(e, groups, stride=PITCH_A), :].T.astype(jnp.bfloat16)
+    def encode(block, carry):
+        first = block * TOGETHER
+        normed = jnp.concatenate(
+            [stage_a[pl.ds(first + k, groups, stride=PITCH_A), :].T for k in range(TOGETHER)],
+            axis=0,
+        ).astype(jnp.bfloat16)
         base = jnp.dot(normed, enc_in[...], preferred_element_type=jnp.float32).astype(jnp.bfloat16)
         middle = silu(jnp.dot(base, enc_mid[...], preferred_element_type=jnp.float32))
         out = base.astype(jnp.float32) + jnp.dot(
             middle.astype(jnp.bfloat16), enc_out[...], preferred_element_type=jnp.float32
         )
-        latent_o[e] = out.astype(jnp.bfloat16)
-        return carry
-
-    lax.fori_loop(0, samples, encode, 0)
+        latent_o[pl.ds(first, TOGETHER)] = out.astype(jnp.bfloat16).reshape(TOGETHER, nodes, -1)
+        return carry
+
+    lax.fori_loop(0, samples // TOGETHER, encode, 0)
 
     def regrid_back(batch, carry):
         for j in range(BATCH):

time: 45.3 us -> 40.9 us (0.903)
  Pallas kernels: 44.5 us -> 40.2 us
    pallas_call x1, Pallas kernels: 42.3 us -> 38 us  [shards(): pl.pallas_call(functools.partial(main_body, groups), out_shape=[pltpu.VME...]
where the time goes in v3:
time: 40.9 us
  Pallas kernels  40.2 us (98%)
  between operations  0.64 us (2%)
    pallas_call x1, Pallas kernels, shards(): pl.pallas_call(functools.partial(main_body, groups), out_shape=[pltpu.VME...  38 us
    pallas_call x1, Pallas kernels, shards(): pl.pallas_call(finish_body, out_shape=[pltpu.HBM(latent_a.shape, bf16), p...  2.25 us

profile of v3, /device:TPU:1, one launch (start us, length us, event | category | flops | bytes accessed | tf_op | source)
XLA Modules:
  0.0 40.9 jit_solution(9102669982126303125)
XLA Ops:
  0.6 38.0 %main.1 = (bf16[16,128,512]{2,1,0:T(8,128)(2,1)S(1)}, bf16[128,32,128]{2,1,0:T(8,128)(2,1)S(1)}) custom-call(s32[256]{0:T(256)} %bitcast.11, bf16[2,256,8,128]{3,2,1,0:T(8,128)(2,1)} %bitcast.10, bf16[128,128,128]{2,1,0:T(8,128)(2,1)} %bitcast.9, bf16[16,128,512]{2,1,0:T(8,128)(2,1)} %latent_h.1, f32[128]{0:T(128)} %norm_a_h.1, bf16[128,512]{1,0:T(8,128)(2,1)} %enc_in_h.1, ...), custom_call_target="tpu_custom_call" | custom-call | tf_op jit(solution)/shard_map/main/pallas_call | solution.py:324
  38.6 2.3 %finish.1 = (bf16[16,128,512]{2,1,0:T(8,128)(2,1)}, bf16[16,32768]{1,0:T(8,128)(2,1)}) custom-call(s32[256]{0:T(256)} %bitcast.12, bf16[16,128,512]{2,1,0:T(8,128)(2,1)S(1)} %get-tuple-element.6.latent, bf16[128,32,128]{2,1,0:T(8,128)(2,1)S(1)} %get-tuple-element.7.cells), custom_call_target="tpu_custom_call" | custom-call | tf_op jit(solution)/shard_map/finish/pallas_call | solution.py:361

commit v4 on v3

--- a/solution.py
+++ b/solution.py
@@ -1,4 +1,5 @@
 import functools
+import itertools
 
 import jax
 import jax.numpy as jnp
@@ -15,12 +16,18 @@
 CHUNK = 16
 PITCH_A = 24
 PITCH_B = 136
+BOX = (4, 2, 8, 2)
+WAYS = sorted(
+    itertools.product(*map(range, BOX)),
+    key=lambda way: -sum(min(k, size - k) for k, size in zip(way[:3], (4, 4, 8))),
+)
 NT = (((1,), (1,)), ((), ()))
 MESH = pl.DeviceIdType.MESH
 
 
 in_hbm = functools.partial(pltpu.with_memory_space_constraint, memory_space=pltpu.HBM)
 in_vmem = functools.partial(pltpu.with_memory_space_constraint, memory_space=pltpu.VMEM)
+in_smem = functools.partial(pltpu.with_memory_space_constraint, memory_space=pltpu.SMEM)
 
 
 def silu(v):
@@ -99,12 +106,19 @@
 
     barrier = pltpu.get_barrier_semaphore()
 
-    def greet(step, carry):
-        peer = {"ch": lax.rem(me + step, groups)}
-        pl.semaphore_signal(barrier, inc=1, device_id=peer, device_id_type=MESH)
-        return carry
-
-    lax.fori_loop(1, groups, greet, 0, unroll=8)
+    x, y = me // (groups // BOX[0]), lax.rem(me // (BOX[2] * BOX[3]), BOX[1])
+    z, core = lax.rem(me // BOX[3], BOX[2]), lax.rem(me, BOX[3])
+    place, step = (x, y, z, core), (groups // BOX[0], BOX[2] * BOX[3], BOX[3], 1)
+    parts = [
+        [lax.rem(place[axis] + k, BOX[axis]) * step[axis] for k in range(BOX[axis])]
+        for axis in range(4)
+    ]
+    planes = [[first + second for second in parts[1]] for first in parts[0]]
+    lines = [[first + second for second in parts[3]] for first in parts[2]]
+    for dx, dy, dz, dc in WAYS:
+        if dx or dy or dz or dc:
+            peer = {"ch": planes[dx][dy] + lines[dz][dc]}
+            pl.semaphore_signal(barrier, inc=1, device_id=peer, device_id_type=MESH)
 
     left_half = lax.broadcasted_iota(jnp.int32, (samples, BC), 1) < BN
 
@@ -266,23 +280,24 @@
         pltpu.make_async_copy(sent.at[most], got.at[most], send_sem).wait()
 
 
-def finish_body(tiles_h, latent, cells, latent_o, cells_o, tiles, tiles_sem, latent_sem, cells_sem):
-    load = pltpu.make_async_copy(tiles_h, tiles, tiles_sem)
-    load.start()
-    whole = pltpu.make_async_copy(latent, latent_o, latent_sem)
-    whole.start()
-    load.wait()
+def finish_body(tiles, latent, cells, latent_o, cells_o, placed, sem):
+    copies = [pltpu.make_async_copy(latent, latent_o, sem.at[0])]
+    copies[0].start()
+    parts, rows = placed.shape[0], placed.shape[2]
 
     def place(s, carry):
         for half in range(2):
-            to = pl.ds(pl.multiple_of(tiles[2 * s + half] * BC, BC), BC)
-            rows = pl.ds(half * latent.shape[0], latent.shape[0])
-            pltpu.make_async_copy(cells.at[s, rows], cells_o.at[:, to], cells_sem).start()
+            to = tiles[2 * s + half]
+            for part in range(parts):
+                first = (half * parts + part) * rows
+                placed[part, to] = cells[s, first : first + rows]
         return carry
 
     lax.fori_loop(0, cells.shape[0], place, 0, unroll=8)
-    pltpu.make_async_copy(cells_o, cells_o, cells_sem).wait()
-    whole.wait()
+    copies.append(pltpu.make_async_copy(placed, cells_o, sem.at[1]))
+    copies[1].start()
+    for copy in copies:
+        copy.wait()
 
 
 def shards(
@@ -320,17 +335,18 @@
     )
     hbm = pl.BlockSpec(memory_space=pltpu.HBM)
     vmem = pl.BlockSpec(memory_space=pltpu.VMEM)
+    smem = pl.BlockSpec(memory_space=pltpu.SMEM)
     message = pltpu.VMEM((groups, samples, nodes), bf16)
-    latent_a, cells = pl.pallas_call(
+    latent_a, cells, tiles = pl.pallas_call(
         functools.partial(main_body, groups),
         out_shape=[
             pltpu.VMEM((samples, nodes, hidden), bf16),
             pltpu.VMEM((groups, 2 * samples, BC), bf16),
+            pltpu.SMEM(tiles.shape, jnp.int32),
         ],
         in_specs=[hbm] * 11,
-        out_specs=[vmem] * 2,
+        out_specs=[vmem, vmem, smem],
         scratch_shapes=[
-            pltpu.SMEM(tiles.shape, jnp.int32),
             pltpu.SMEM(norm_a.shape, f32),
             pltpu.VMEM(fields.shape, bf16),
             pltpu.VMEM(regrid.shape, bf16),
@@ -362,19 +378,17 @@
         finish_body,
         out_shape=[
             pltpu.HBM(latent_a.shape, bf16),
-            pltpu.HBM((samples, all_cells), bf16),
+            pltpu.HBM(fields.shape, bf16),
         ],
-        in_specs=[hbm, vmem, vmem],
+        in_specs=[smem, vmem, vmem],
         out_specs=[hbm, hbm],
         scratch_shapes=[
-            pltpu.SMEM(tiles.shape, jnp.int32),
-            pltpu.SemaphoreType.DMA,
-            pltpu.SemaphoreType.DMA,
-            pltpu.SemaphoreType.DMA,
+            pltpu.VMEM(fields.shape, bf16),
+            pltpu.SemaphoreType.DMA((2,)),
         ],
         name="finish",
-    )(in_hbm(tiles), in_vmem(latent_a), in_vmem(cells))
-    return latent_a, cells_b.reshape(samples, 1, all_cells)
+    )(in_smem(tiles), in_vmem(latent_a), in_vmem(cells))
+    return latent_a, jnp.swapaxes(cells_b, 1, 2).reshape(samples, 1, all_cells)
 
 
 def solution(mesh):

time: 40.9 us -> 40.1 us (0.980)
  Pallas kernels: 40.2 us -> 39.4 us
    pallas_call x1, Pallas kernels: 2.25 us -> 1.68 us  [shards(): pl.pallas_call(finish_body, out_shape=[pltpu.HBM(latent_a.shape, bf16), p...]
where the time goes in v4:
time: 40.1 us; the launch traced here: 40 us
  Pallas kernels  39.4 us (98%)
  between operations  0.64 us (2%)
    pallas_call x1, Pallas kernels, shards(): pl.pallas_call(functools.partial(main_body, groups), out_shape=[pltpu.VME...  37.7 us
    pallas_call x1, Pallas kernels, shards(): pl.pallas_call(finish_body, out_shape=[pltpu.HBM(latent_a.shape, bf16), p...  1.68 us

profile of v4, /device:TPU:1, one launch (start us, length us, event | category | flops | bytes accessed | tf_op | source)
XLA Modules:
  0.0 40.0 jit_solution(17918625527398535050)
XLA Ops:
  0.6 37.7 %main.1 = (bf16[16,128,512]{2,1,0:T(8,128)(2,1)S(1)}, bf16[128,32,128]{2,1,0:T(8,128)(2,1)S(1)}, s32[256]{0:T(256)S(4)}) custom-call(s32[256]{0:T(256)} %bitcast.14, bf16[2,256,8,128]{3,2,1,0:T(8,128)(2,1)} %bitcast.12, bf16[128,128,128]{2,1,0:T(8,128)(2,1)} %bitcast.11, bf16[16,128,512]{2,1,0:T(8,128)(2,1)} %latent_h.1, f32[128]{0:T(128)} %norm_a_h.1, ...), custom_call_target="tpu_custom_call" | custom-call | tf_op jit(solution)/shard_map/main/pallas_call | solution.py:340
  38.4 1.7 %finish.1 = (bf16[16,128,512]{2,1,0:T(8,128)(2,1)}, bf16[2,256,8,128]{3,2,1,0:T(8,128)(2,1)}) custom-call(s32[256]{0:T(256)S(4)} %get-tuple-element.7.tiles, bf16[16,128,512]{2,1,0:T(8,128)(2,1)S(1)} %get-tuple-element.8.latent, bf16[128,32,128]{2,1,0:T(8,128)(2,1)S(1)} %get-tuple-element.9.cells), custom_call_target="tpu_custom_call" | custom-call | tf_op jit(solution)/shard_map/finish/pallas_call | solution.py:377

commit v5 on v4

--- a/solution.py
+++ b/solution.py
@@ -14,6 +14,7 @@
 BATCH = 8
 TOGETHER = 4
 CHUNK = 16
+EARLY = 1
 PITCH_A = 24
 PITCH_B = 136
 BOX = (4, 2, 8, 2)
@@ -63,6 +64,7 @@
     dec_out,
     sent_a,
     sent_b,
+    early_b,
     got_a,
     got_b,
     stage_a,
@@ -138,7 +140,45 @@
         return one
 
     send_a = send(sent_a, got_a, lambda step: recv_a)
-    send_b = send(sent_b, got_b, lambda step: recv_b.at[step // BATCH])
+    def copy_b(src, peer, step):
+        pltpu.make_async_remote_copy(
+            src_ref=src,
+            dst_ref=got_b.at[me],
+            send_sem=send_sem,
+            recv_sem=recv_b.at[step // BATCH],
+            device_id={"ch": peer},
+            device_id_type=MESH,
+        ).start()
+
+    def send_b(step, carry):
+        peer = lax.rem(me + step, groups)
+
+        @pl.when(lax.rem(peer // BOX[3], BOX[2]) >= EARLY)
+        def _():
+            copy_b(sent_b.at[peer], peer, step)
+
+        return carry
+
+    per_layer = groups // BOX[2]
+    place_in_layer = me // (BOX[2] * BOX[3]) * BOX[3] + core
+
+    def early(k):
+        there = lax.rem(place_in_layer + k % per_layer, per_layer)
+        layer = k // per_layer
+        return (there // BOX[3] * BOX[2] + layer) * BOX[3] + lax.rem(there, BOX[3])
+
+    def pack_early(batch):
+        for k in range(batch * BATCH, (batch + 1) * BATCH):
+            rows = stage_b[pl.ds(early(k), samples, stride=PITCH_B), :]
+            early_b[k] = rows.astype(jnp.bfloat16)
+
+    def send_early(batch):
+        for k in range(batch * BATCH, (batch + 1) * BATCH):
+            peer = early(k)
+
+            @pl.when(peer != me)
+            def _(k=k, peer=peer):
+                copy_b(early_b.at[k], peer, lax.rem(peer + groups - me, groups))
 
     def regrid_batch(batch):
         for j in range(BATCH):
@@ -205,7 +245,13 @@
             send_b((batch - 1) * BATCH + j, carry)
         return carry
 
+    early_batches = EARLY * per_layer // BATCH
+    pack_early(0)
+    for batch in range(1, early_batches):
+        pack_early(batch)
+        send_early(batch - 1)
     pack_batch(0, 0)
+    send_early(early_batches - 1)
     pack_batch(1, 0)
     lax.fori_loop(1, BATCH, send_b, 0, unroll=True)
     lax.fori_loop(2, batches, pack_and_send, 0)
@@ -359,6 +405,7 @@
             pltpu.VMEM(dec_out.shape, bf16),
             message,
             message,
+            pltpu.VMEM((EARLY * groups // BOX[2], samples, nodes), bf16),
             message,
             message,
             pltpu.VMEM((groups * PITCH_A, nodes), f32),

time: 40.1 us -> 38.5 us (0.960)
  the two profiles are of different devices: /device:TPU:1 before, /device:TPU:33 now
where the time goes in v5:
time: 38.5 us; the launch traced here: 38.4 us
  Pallas kernels  37.8 us (98%)
  between operations  0.64 us (2%)
    pallas_call x1, Pallas kernels, shards(): pl.pallas_call(functools.partial(main_body, groups), out_shape=[pltpu.VME...  36.1 us
    pallas_call x1, Pallas kernels, shards(): pl.pallas_call(finish_body, out_shape=[pltpu.HBM(latent_a.shape, bf16), p...  1.68 us

profile of v5, /device:TPU:33, one launch (start us, length us, event | category | flops | bytes accessed | tf_op | source)
XLA Modules:
  0.0 38.4 jit_solution(17196958675268672482)
XLA Ops:
  0.6 36.1 %main.1 = (bf16[16,128,512]{2,1,0:T(8,128)(2,1)S(1)}, bf16[128,32,128]{2,1,0:T(8,128)(2,1)S(1)}, s32[256]{0:T(256)S(4)}) custom-call(s32[256]{0:T(256)} %bitcast.14, bf16[2,256,8,128]{3,2,1,0:T(8,128)(2,1)} %bitcast.12, bf16[128,128,128]{2,1,0:T(8,128)(2,1)} %bitcast.11, bf16[16,128,512]{2,1,0:T(8,128)(2,1)} %latent_h.1, f32[128]{0:T(128)} %norm_a_h.1, ...), custom_call_target="tpu_custom_call" | custom-call | tf_op jit(solution)/shard_map/main/pallas_call | solution.py:386
  36.7 1.7 %finish.1 = (bf16[16,128,512]{2,1,0:T(8,128)(2,1)}, bf16[2,256,8,128]{3,2,1,0:T(8,128)(2,1)}) custom-call(s32[256]{0:T(256)S(4)} %get-tuple-element.7.tiles, bf16[16,128,512]{2,1,0:T(8,128)(2,1)S(1)} %get-tuple-element.8.latent, bf16[128,32,128]{2,1,0:T(8,128)(2,1)S(1)} %get-tuple-element.9.cells), custom_call_target="tpu_custom_call" | custom-call | tf_op jit(solution)/shard_map/finish/pallas_call | solution.py:424

commit v6 on v5

--- a/solution.py
+++ b/solution.py
@@ -246,15 +246,15 @@
         return carry
 
     early_batches = EARLY * per_layer // BATCH
-    pack_early(0)
-    for batch in range(1, early_batches):
-        pack_early(batch)
-        send_early(batch - 1)
     pack_batch(0, 0)
-    send_early(early_batches - 1)
     pack_batch(1, 0)
     lax.fori_loop(1, BATCH, send_b, 0, unroll=True)
-    lax.fori_loop(2, batches, pack_and_send, 0)
+    lax.fori_loop(2, 4, pack_and_send, 0)
+    for batch in range(early_batches):
+        pack_early(batch)
+    for batch in range(early_batches):
+        send_early(batch)
+    lax.fori_loop(4, batches, pack_and_send, 0)
     lax.fori_loop(groups - BATCH, groups, send_b, 0, unroll=True)
     got_b[me] = sent_b[me]
 

time: 38.5 us -> 38.5 us (level)
  no operation moved by 1% of the time
where the time goes in v6:
time: 38.5 us; the launch traced here: 38.4 us
  Pallas kernels  37.8 us (98%)
  between operations  0.64 us (2%)
    pallas_call x1, Pallas kernels, shards(): pl.pallas_call(functools.partial(main_body, groups), out_shape=[pltpu.VME...  36.1 us
    pallas_call x1, Pallas kernels, shards(): pl.pallas_call(finish_body, out_shape=[pltpu.HBM(latent_a.shape, bf16), p...  1.68 us

profile of v6, /device:TPU:33, one launch (start us, length us, event | category | flops | bytes accessed | tf_op | source)
XLA Modules:
  0.0 38.4 jit_solution(11072956495821295434)
XLA Ops:
  0.6 36.1 %main.1 = (bf16[16,128,512]{2,1,0:T(8,128)(2,1)S(1)}, bf16[128,32,128]{2,1,0:T(8,128)(2,1)S(1)}, s32[256]{0:T(256)S(4)}) custom-call(s32[256]{0:T(256)} %bitcast.14, bf16[2,256,8,128]{3,2,1,0:T(8,128)(2,1)} %bitcast.12, bf16[128,128,128]{2,1,0:T(8,128)(2,1)} %bitcast.11, bf16[16,128,512]{2,1,0:T(8,128)(2,1)} %latent_h.1, f32[128]{0:T(128)} %norm_a_h.1, ...), custom_call_target="tpu_custom_call" | custom-call | tf_op jit(solution)/shard_map/main/pallas_call | solution.py:386
  36.7 1.7 %finish.1 = (bf16[16,128,512]{2,1,0:T(8,128)(2,1)}, bf16[2,256,8,128]{3,2,1,0:T(8,128)(2,1)}) custom-call(s32[256]{0:T(256)S(4)} %get-tuple-element.7.tiles, bf16[16,128,512]{2,1,0:T(8,128)(2,1)S(1)} %get-tuple-element.8.latent, bf16[128,32,128]{2,1,0:T(8,128)(2,1)S(1)} %get-tuple-element.9.cells), custom_call_target="tpu_custom_call" | custom-call | tf_op jit(solution)/shard_map/finish/pallas_call | solution.py:424
